TPU v7x, 256 devices: a whole 4x4x8 slice. The times are simulated.
256 devices in a mesh: seq: 32 (over y, z), batch: 8 (over x, core).
Axes of the slice: x: 4, y: 4, z: 8, core: 2. Of those that a mesh axis runs over, the one named last changes fastest.
Arguments:
- conv_input: bfloat16 [32768, 8192], P(('batch', 'seq')), parts along dimension 0, may hold values from -6 to 6
- gate_input: bfloat16 [32768, 8192], P(('batch', 'seq')), parts along dimension 0, may hold values from -6 to 6
- conv_weight: bfloat16 [4, 8192], P(None, 'seq'), may hold values from -3 to 3
- conv_bias: bfloat16 [8192], P('seq'), may hold values from -3 to 3
- x_weight: bfloat16 [8192, 288], P('seq'), may hold values from -0.0625 to 0.0625
- dt_gain: float32 [256], replicated, may hold values from 0.5 to 1.5
- dt_weight: bfloat16 [256, 8192], P(None, 'seq'), may hold values from -0.375 to 0.375
- dt_bias: float32 [8192], P('seq'), may hold values from -6.9 to -2.3
- a_log: float32 [16, 8192], P(None, 'seq'), may hold values from 0 to 2.77
- skip: float32 [8192], P('seq'), may hold values from 0.5 to 1.5
Outputs:
- mixed: bfloat16 [32768, 8192], P(('batch', 'seq')), parts along dimension 0
There are 8 independent parts, one for each index of `batch`. A program takes and returns all parts, laid end to end along the dimension named above; an argument that names none is the same for every part. Nothing has to cross between parts.
All inputs are finite; a program needn't handle non-finite values.
Results may differ from a plain program's by a relative error of at most 0.0085.
Values may be sent and summed in bfloat16 or wider, within the bound.
A program may use at most 128 MiB of HBM per device.

v0:
```python
import jax
import jax.numpy as jnp
from jax import lax
from jax.sharding import PartitionSpec as P


def passed_along(value, axis, steps):
    count = lax.axis_size(axis)
    initial, last = (max(0, -steps), min(count, count - steps))
    return lax.ppermute(value, axis, [(source, source + steps) for source in range(initial, last)])


def from_everyone(x, axis):
    copies = jnp.broadcast_to(x, (lax.axis_size(axis), *x.shape))
    return lax.all_to_all(copies, axis, split_axis=0, concat_axis=0, tiled=True)


def joined_along(parts, dim):
    parts = jnp.moveaxis(parts, 0, dim)
    dims = parts.shape
    return parts.reshape(*dims[:dim], dims[dim] * dims[dim + 1], *dims[dim + 2 :])


def gather_directly(x, axis, dim):
    parts = from_everyone(x, axis)
    return joined_along(parts, dim)


def causal_conv(prefix, inputs, weight, bias):
    rows = inputs.shape[0]
    width = weight.shape[0]
    padded = jnp.concatenate([prefix, inputs.astype(jnp.float32)], 0)
    total = bias.astype(jnp.float32)[None, :]
    for tap in range(width):
        total = total + weight[tap].astype(jnp.float32)[None, :] * padded[tap : tap + rows]
    return jax.nn.silu(total).astype(jnp.bfloat16)


def link_blocks(earlier, later):
    return (earlier[0] * later[0], later[0] * earlier[1] + later[1])


def selective_scan(step, xfloat, bmat, cmat, rate):
    span = 16
    length, chans = step.shape
    states = rate.shape[0]
    blocks = length // span
    step_rows = step.reshape(blocks, span * chans)
    drive_rows = (step * xfloat).reshape(blocks, span * chans)
    b_rows = bmat.reshape(blocks, span * states)
    c_rows = cmat.reshape(blocks, span * states)
    state = jnp.zeros((blocks, states, chans), jnp.float32)
    running = jnp.zeros((blocks, chans), jnp.float32)
    local_parts = []
    elapsed = []
    for place in range(span):
        step_now = step_rows[:, place * chans : (place + 1) * chans]
        drive_now = drive_rows[:, place * chans : (place + 1) * chans]
        b_now = b_rows[:, place * states : (place + 1) * states]
        c_now = c_rows[:, place * states : (place + 1) * states]
        state = (
            jnp.exp(step_now[:, None, :] * rate[None]) * state
            + b_now[:, :, None] * drive_now[:, None, :]
        )
        local_parts.append(jnp.sum(c_now[:, :, None] * state, axis=1))
        running = running + step_now
        elapsed.append(running)
    totals = jnp.exp(running[:, None, :] * rate[None])
    _, through = lax.associative_scan(link_blocks, (totals, state), axis=0)
    starts = jnp.concatenate([jnp.zeros((1, states, chans), jnp.float32), through[: blocks - 1]], 0)
    pieces = []
    for place in range(span):
        c_now = c_rows[:, place * states : (place + 1) * states]
        carried = jnp.sum(
            c_now[:, :, None] * jnp.exp(elapsed[place][:, None, :] * rate[None]) * starts, axis=1
        )
        pieces.append(local_parts[place] + carried)
    return jnp.concatenate(pieces, 1).reshape(length, chans)


def local(
    conv_input,
    gate_input,
    conv_weight,
    conv_bias,
    x_weight,
    dt_gain,
    dt_weight,
    dt_bias,
    a_log,
    skip,
):
    width = conv_weight.shape[0]
    rank = dt_weight.shape[0]
    states = a_log.shape[0]
    prior = passed_along(conv_input[conv_input.shape[0] - (width - 1) :], "seq", 1)
    params = gather_directly(jnp.concatenate([conv_weight, conv_bias[None, :]], 0), "seq", 1)
    outgoing = causal_conv(prior.astype(jnp.float32), conv_input, params[:width], params[width])
    local_proj = jnp.dot(
        outgoing,
        lax.all_gather(x_weight, "seq", axis=0, tiled=True),
        preferred_element_type=jnp.float32,
    )
    arrived, gate_part = (
        lax.all_to_all(outgoing, "seq", split_axis=1, concat_axis=0, tiled=True),
        lax.all_to_all(gate_input, "seq", split_axis=1, concat_axis=0, tiled=True),
    )
    proj = lax.all_gather(local_proj, "seq", axis=0, tiled=True)
    dt_low = proj[:, :rank]
    bmat = proj[:, rank : rank + states]
    cmat = proj[:, rank + states :]
    normed = (
        dt_low
        * lax.rsqrt(jnp.mean(dt_low * dt_low, axis=1, keepdims=True) + 1e-06)
        * dt_gain[None, :]
    ).astype(jnp.bfloat16)
    step = jax.nn.softplus(
        jnp.dot(normed, dt_weight, preferred_element_type=jnp.float32) + dt_bias[None, :]
    )
    rate = -jnp.exp(a_log)
    xfloat = arrived.astype(jnp.float32)
    scanned = selective_scan(step, xfloat, bmat, cmat, rate)
    y_out = (scanned + skip[None, :] * xfloat).astype(jnp.bfloat16)
    held = lax.optimization_barrier(y_out)
    gated = (held.astype(jnp.float32) * jax.nn.silu(gate_part.astype(jnp.float32))).astype(
        jnp.bfloat16
    )
    return lax.all_to_all(gated, "seq", split_axis=0, concat_axis=1, tiled=True)


def solution(mesh):
    return jax.shard_map(
        local,
        mesh=mesh,
        in_specs=(
            P(("batch", "seq"), None),
            P(("batch", "seq"), None),
            P(None, "seq"),
            P("seq"),
            P("seq", None),
            P(),
            P(None, "seq"),
            P("seq"),
            P(None, "seq"),
            P("seq"),
        ),
        out_specs=P(("batch", "seq"), None),
        check_vma=False,
    )
```

profile of v0, /device:TPU:32, one launch (start us, length us, event | category | flops | bytes accessed | tf_op | source)
XLA Modules:
  0.0 660.3 jit_solution(11097169348318939079)
XLA Ops:
  9.3 11.4 %all-to-all-start = ((bf16[32,5,256]{2,1,0:T(8,128)(2,1)}), bf16[32,5,256]{2,1,0:T(8,128)(2,1)S(1)}, u32[]{:S(2)}, u32[]{:S(2)}) async-start(bf16[32,5,256]{2,1,0:T(8,128)(2,1)} %broadcast_in_dim.7), calls=%async_computation | async-start | bytes 262144 | tf_op jit(solution)/shard_map/all_to_all | solution.py:15
  21.6 3.4 collective-permute-start
  25.0 4.1 convert_element_type.94
  30.5 7.6 %multiply_convert_fusion.1 = bf16[128,8192]{1,0:T(8,128)(2,1)S(1)} fusion(f32[128,8192]{1,0:T(8,128)} %convert_element_type.94, f32[3,8192]{1,0:T(4,128)S(1)} %convert_element_type.93, f32[8192]{0:T(1024)S(1)} %bitcast.55, f32[8192]{0:T(1024)S(1)} %bitcast.56, f32[8192]{0:T(1024)S(1)} %bitcast.57, f32[8192]{0:T(1024)S(1)} %bitcast.58, f32[8192]{0:T(1024)S(1)} %bitcast.54), kind=kLoop, calls=%fused_computation.78 | loop fusion | flops 16777216 | bytes 6553600 | tf_op jit(solution)/shard_map/convert_element_type | solution.py:36
  38.2 59.4 %all-gather.3.cloned.1.call-done = bf16[8192,288]{0,1:T(8,128)(2,1)} async-done(((bf16[256,288]{0,1:T(8,128)(2,1)}), bf16[8192,288]{0,1:T(8,128)(2,1)}) %all-gather.3.cloned.1.call-update) | async-done | bytes 4718608 | tf_op jit(solution)/shard_map/all_gather | solution.py:101
  97.5 4.4 fusion.36
  103.5 9.4 %all-to-all-start.1 = ((bf16[128,32,256]{2,0,1:T(8,128)(2,1)}), bf16[128,32,256]{2,0,1:T(8,128)(2,1)S(1)}, u32[]{:S(2)}, u32[]{:S(2)}) async-start(bf16[128,32,256]{2,0,1:T(8,128)(2,1)} %bitcast.50), calls=%async_computation.1 | async-start | bytes 4194304 | tf_op jit(solution)/shard_map/all_to_all | solution.py:105
  113.0 3.2 copy.29
  116.2 88.2 %all-gather.5.cloned.1.call-done = f32[4096,288]{0,1:T(8,128)} async-done(((f32[128,288]{0,1:T(8,128)}), f32[4096,288]{0,1:T(8,128)}) %all-gather.5.cloned.1.call-update) | async-done | bytes 4718608 | tf_op jit(solution)/shard_map/all_gather | solution.py:108
  204.4 2.5 multiply_reduce_fusion.32
  206.9 9.4 %all-to-all-start.2 = ((bf16[128,32,256]{2,0,1:T(8,128)(2,1)}), bf16[128,32,256]{2,0,1:T(8,128)(2,1)}, u32[]{:S(2)}, u32[]{:S(2)}) async-start(bf16[128,32,256]{2,0,1:T(8,128)(2,1)} %bitcast.49), calls=%async_computation.2 | async-start | bytes 4194304 | tf_op jit(solution)/shard_map/all_to_all | solution.py:106
  216.4 8.7 %bitcast_multiply_fusion.2 = (f32[4096,256]{1,0:T(8,128)}, f32[4096,256]{1,0:T(8,128)}) fusion(bf16[128,32,256]{2,0,1:T(8,128)(2,1)S(1)} %all-to-all-done.1, f32[256]{0:T(256)S(1)} %copy-done.131, bf16[256,256]{1,0:T(8,128)(2,1)S(1)} %copy-done, f32[4096,288]{0,1:T(8,128)} %all-gather.5.cloned.1.call-done, f32[256]{0:T(256)S(1)} %copy-done.132, ...), kind=kOutput, calls=%fused_computation.23 | convolution fusion | flops 549453824 | bytes 14829568 | tf_op jit(solution)/shard_map/dot_general | solution.py:118
  225.1 5.0 reshape.167
  230.1 4.4 slice_add_fusion.22
  236.4 5.0 reshape.169
  241.4 4.0 fusion.30
  254.2 20.0 %multiply_reduce_fusion.1 = (f32[256,256]{1,0:T(8,128)}, f32[256,16,256]{2,1,0:T(8,128)S(1)}, f32[256,16,256]{2,1,0:T(8,128)S(1)}, f32[256,16,256]{2,1,0:T(8,128)}) fusion(f32[256,16]{1,0:T(8,128)S(1)} %get-tuple-element.99, f32[256,256]{1,0:T(8,128)} %get-tuple-element.77, f32[256,16]{1,0:T(8,128)} %get-tuple-element.117, ...), kind=kLoop, calls=%fused_computation.27 | loop fusion | flops 69140480 | bytes 21528576 | tf_op jit(solution)/shard_map/reduce_sum | solution.py:65
  274.2 6.4 multiply_reduce_fusion.3
  288.2 2.0 pad.53
  291.5 1.9 pad.52
  298.6 3.3 pad.55
  307.0 2.9 pad.57
  310.8 3.1 pad.56
  317.6 5.6 pad.58
  323.2 8.7 %pad.59 = f32[32,16,256]{2,1,0:T(8,128)} pad(f32[16,16,256]{2,1,0:T(8,128)} %add.351, f32[]{:T(128)} %constant.5.clone.1), padding=1_0_1x0_0_0x0_0_0 | pad | bytes 786436 | tf_op jit(solution)/shard_map/pad | solution.py:69
  331.9 2.1 add.353
  334.0 2.3 fusion.20
  336.3 11.6 %pad.61 = f32[64,16,256]{2,1,0:T(8,128)S(1)} pad(f32[32,16,256]{2,1,0:T(8,128)} %add.353, f32[]{:T(128)} %constant.5.clone.1), padding=1_0_1x0_0_0x0_0_0 | pad | bytes 1572868 | tf_op jit(solution)/shard_map/pad | solution.py:69
  349.8 15.6 %pad.60 = f32[64,16,256]{2,1,0:T(8,128)} pad(f32[32,16,256]{2,1,0:T(8,128)} %pad_maximum_fusion.3, f32[]{:T(128)} %constant.5.clone.1), padding=0_1_1x0_0_0x0_0_0 | pad | bytes 1572868 | tf_op jit(solution)/shard_map/pad | solution.py:69
  365.4 2.1 fusion.19
  369.8 23.1 %pad.62 = f32[128,16,256]{2,1,0:T(8,128)S(1)} pad(f32[64,16,256]{2,1,0:T(8,128)} %pad_maximum_fusion.2, f32[]{:T(128)} %constant.5.clone.1), padding=0_1_1x0_0_0x0_0_0 | pad | bytes 3145732 | tf_op jit(solution)/shard_map/pad | solution.py:69
  392.9 20.5 %pad.63 = f32[128,16,256]{2,1,0:T(8,128)} pad(f32[64,16,256]{2,1,0:T(8,128)S(1)} %copy-done.14, f32[]{:T(128)} %constant.5.clone.1), padding=1_0_1x0_0_0x0_0_0 | pad | bytes 3145732 | tf_op jit(solution)/shard_map/pad | solution.py:69
  413.4 3.5 add.357
  417.6 4.1 fusion.18
  422.5 9.2 %multiply_reduce_fusion.17 = f32[256,256]{1,0:T(8,128)} fusion(f32[256,16]{1,0:T(8,128)S(1)} %copy-done.103, f32[256,256]{1,0:T(8,128)S(1)} %copy-done.93, f32[256,16]{1,0:T(8,128)S(1)} %copy-done.128, f32[256,256]{1,0:T(8,128)S(1)} %copy-done.102, f32[16,256]{1,0:T(8,128)S(1)} %exponential_negate_fusion, f32[256,256]{1,0:T(8,128)S(1)} %copy-done.92, ...), kind=kLoop, calls=%fused_computation.43 | loop fusion | flops 35586048 | bytes 4620288 | tf_op jit(solution)/shard_map/reduce_sum | solution.py:65
  431.7 40.5 %pad.161 = f32[256,16,256]{2,1,0:T(8,128)} pad(f32[128,16,256]{2,1,0:T(8,128)S(1)} %copy-done.11, f32[]{:T(128)} %constant.5.clone.1), padding=1_0_1x0_0_0x0_0_0 | pad | bytes 6291460
  473.9 40.5 %pad.87 = f32[255,16,256]{2,1,0:T(8,128)} pad(f32[128,16,256]{2,1,0:T(8,128)S(1)} %pad_maximum_fusion.1, f32[]{:T(128)} %constant.5.clone.1), padding=0_0_1x0_0_0x0_0_0 | pad | bytes 6275076 | tf_op jit(solution)/shard_map/slice | solution.py:70
  514.5 8.7 %multiply_reduce_fusion.19 = f32[256,256]{1,0:T(8,128)S(1)} fusion(f32[256,16]{1,0:T(8,128)S(1)} %copy-done.105, f32[256,256]{1,0:T(8,128)} %get-tuple-element.86, f32[256,16]{1,0:T(8,128)} %get-tuple-element.126, f32[256,256]{1,0:T(8,128)} %get-tuple-element.87, f32[256,16]{1,0:T(8,128)} %get-tuple-element.127, f32[256,256]{1,0:T(8,128)} %get-tuple-element.65, ...), kind=kLoop, calls=%fused_computation.45 | loop fusion | flops 31391744 | bytes 4079616 | tf_op jit(solution)/shard_map/reduce_sum | solution.py:65
  523.4 6.3 multiply_reduce_fusion.21
  531.2 9.1 %multiply_reduce_fusion.29 = (f32[256,256]{1,0:T(8,128)S(1)}, f32[256,256]{1,0:T(8,128)S(1)}, f32[256,256]{1,0:T(8,128)S(1)}, f32[256,256]{1,0:T(8,128)S(1)}, f32[256,256]{1,0:T(8,128)S(1)}, /*index=5*/f32[256,256]{1,0:T(8,128)S(1)}) fusion(f32[256,16]{1,0:T(8,128)S(1)} %copy-done.113, f32[256,256]{1,0:T(8,128)S(1)} %copy-done.87, ...), kind=kLoop, calls=%fused_computation.55 | loop fusion | flops 27918336 | bytes 7716864 | tf_op jit(solution)/shard_map/reduce_sum | solution.py:65
  541.1 7.6 %multiply_reduce_fusion.23 = (f32[256,256]{1,0:T(8,128)S(1)}, f32[256,256]{1,0:T(8,128)S(1)}, f32[256,256]{1,0:T(8,128)S(1)}) fusion(f32[256,16]{1,0:T(8,128)S(1)} %copy-done.110, f32[256,256]{1,0:T(8,128)S(1)} %copy-done.81, f32[256,16]{1,0:T(8,128)S(1)} %copy-done.117, f32[256,256]{1,0:T(8,128)S(1)} %copy-done.84, f32[256,16]{1,0:T(8,128)S(1)} %copy-done.119, ...), kind=kLoop, calls=%fused_computation.49 | loop fusion | flops 27066368 | bytes 3555328 | tf_op jit(solution)/shard_map/reduce_sum | solution.py:65
  548.9 8.8 %multiply_reduce_fusion = (f32[256,256]{1,0:T(8,128)S(1)}, f32[256,256]{1,0:T(8,128)S(1)}, f32[256,256]{1,0:T(8,128)S(1)}, f32[256,256]{1,0:T(8,128)S(1)}, f32[256,256]{1,0:T(8,128)S(1)}, /*index=5*/f32[256,256]{1,0:T(8,128)S(1)}) fusion(f32[256,16]{1,0:T(8,128)S(1)} %copy-done.108, f32[16,256]{1,0:T(8,128)S(1)} %exponential_negate_fusion, ...), kind=kLoop, calls=%fused_computation.26 | loop fusion | flops 24772608 | bytes 7438336 | tf_op jit(solution)/shard_map/reduce_sum | solution.py:74
  561.7 8.8 %multiply_reduce_fusion.2 = (f32[256,256]{1,0:T(8,128)S(1)}, f32[256,256]{1,0:T(8,128)S(1)}, f32[256,256]{1,0:T(8,128)S(1)}, f32[256,256]{1,0:T(8,128)S(1)}, f32[256,256]{1,0:T(8,128)S(1)}, /*index=5*/f32[256,256]{1,0:T(8,128)S(1)}) fusion(f32[256,256]{1,0:T(8,128)S(1)} %copy-done.57, f32[256,16]{1,0:T(8,128)S(1)} %copy-done.50, ...), kind=kLoop, calls=%fused_computation.28 | loop fusion | flops 24772608 | bytes 7438336 | tf_op jit(solution)/shard_map/reduce_sum | solution.py:74
  572.1 7.2 %multiply_reduce_fusion.9 = (f32[256,256]{1,0:T(8,128)S(1)}, f32[256,256]{1,0:T(8,128)S(1)}, f32[256,256]{1,0:T(8,128)S(1)}, f32[256,256]{1,0:T(8,128)S(1)}) fusion(f32[256,16]{1,0:T(8,128)S(1)} %copy-done.46, f32[256,256]{1,0:T(8,128)S(1)} %copy-done.27, f32[256,16]{1,0:T(8,128)S(1)} %copy-done.40, f32[256,256]{1,0:T(8,128)S(1)} %copy-done.37, ...), kind=kLoop, calls=%fused_computation.35 | loop fusion | flops 20709376 | bytes 6946816 | tf_op jit(solution)/shard_map/reduce_sum | solution.py:65
  585.6 4.9 reshape.170
  590.6 3.3 fusion.14
  593.9 2.9 fusion.15
  596.8 55.1 %all_to_all.50 = bf16[32,128,256]{2,1,0:T(8,128)(2,1)S(1)} all-to-all(bf16[32,128,256]{2,1,0:T(8,128)(2,1)S(1)} %bitcast.48), channel_id=1, replica_groups=mesh['seq'=32,'batch'=8] {'seq'}, dimensions={0} | all-to-all | bytes 4194304 | tf_op jit(solution)/shard_map/all_to_all | solution.py:128
  (340 shorter events, 63.3 us)
Async XLA Ops:
  6.5 209.8 %copy-start = (bf16[256,256]{1,0:T(8,128)(2,1)S(1)}, bf16[256,256]{1,0:T(8,128)(2,1)}, u32[]{:S(2)}) copy-start(bf16[256,256]{1,0:T(8,128)(2,1)} %param.16) | copy-start | bytes 393220
  6.5 91.0 %all-gather.3.cloned.1.call-start = ((), (), s32[]{:S(2)}) async-start(), calls=%async_computation.4 | async-start | bytes 4866048 | tf_op jit(solution)/shard_map/all_gather | solution.py:101
  9.3 21.2 %all-to-all-start = ((bf16[32,5,256]{2,1,0:T(8,128)(2,1)}), bf16[32,5,256]{2,1,0:T(8,128)(2,1)S(1)}, u32[]{:S(2)}, u32[]{:S(2)}) async-start(bf16[32,5,256]{2,1,0:T(8,128)(2,1)} %broadcast_in_dim.7), calls=%async_computation | async-start | bytes 262144 | tf_op jit(solution)/shard_map/all_to_all | solution.py:15
  20.6 183.7 %all-gather.5.cloned.1.call-start = ((), (), s32[]{:S(2)}) async-start(), calls=%async_computation.5 | async-start | bytes 4866048 | tf_op jit(solution)/shard_map/all_gather | solution.py:108
  21.6 7.5 %collective-permute-start = (bf16[3,8192]{1,0:T(4,128)(2,1)S(1)}, bf16[3,8192]{1,0:T(4,128)(2,1)S(1)}, u32[]{:S(2)}, u32[]{:S(2)}) collective-permute-start(bf16[3,8192]{1,0:T(4,128)(2,1)S(1)} %slice.443), channel_id=1, source_target_pairs={{0,8},{8,16},{16,24},{24,32},{32,40},{40,48},{48,56},{56,64},{64,7... | collective-permute-start | bytes 147464 | tf_op jit(solution)/shard_map/ppermute | solution.py:10
  103.5 12.6 %copy-start.129 = (f32[16,256]{1,0:T(8,128)S(1)}, f32[16,256]{1,0:T(8,128)}, u32[]{:S(2)}) copy-start(f32[16,256]{1,0:T(8,128)} %param.18) | copy-start | bytes 49156
  103.5 103.4 %all-to-all-start.1 = ((bf16[128,32,256]{2,0,1:T(8,128)(2,1)}), bf16[128,32,256]{2,0,1:T(8,128)(2,1)S(1)}, u32[]{:S(2)}, u32[]{:S(2)}) async-start(bf16[128,32,256]{2,0,1:T(8,128)(2,1)} %bitcast.50), calls=%async_computation.1 | async-start | bytes 4194304 | tf_op jit(solution)/shard_map/all_to_all | solution.py:105
  116.2 100.2 %copy-start.131 = (f32[256]{0:T(256)S(1)}, f32[256]{0:T(256)}, u32[]{:S(2)}) copy-start(f32[256]{0:T(256)} %param.17) | copy-start | bytes 3076
  116.2 100.2 %copy-start.132 = (f32[256]{0:T(256)S(1)}, f32[256]{0:T(256)}, u32[]{:S(2)}) copy-start(f32[256]{0:T(256)} %param.15) | copy-start | bytes 3076
  206.9 18.2 %copy-start.12 = (bf16[128,32,256]{2,0,1:T(8,128)(2,1)}, bf16[128,32,256]{2,0,1:T(8,128)(2,1)S(1)}, u32[]{:S(2)}) copy-start(bf16[128,32,256]{2,0,1:T(8,128)(2,1)S(1)} %all-to-all-done.1) | copy-start | bytes 6291460
  206.9 387.0 %all-to-all-start.2 = ((bf16[128,32,256]{2,0,1:T(8,128)(2,1)}), bf16[128,32,256]{2,0,1:T(8,128)(2,1)}, u32[]{:S(2)}, u32[]{:S(2)}) async-start(bf16[128,32,256]{2,0,1:T(8,128)(2,1)} %bitcast.49), calls=%async_computation.2 | async-start | bytes 4194304 | tf_op jit(solution)/shard_map/all_to_all | solution.py:106
  234.5 39.7 %copy-start.19 = (f32[256,256]{1,0:T(8,128)}, f32[256,256]{1,0:T(8,128)S(1)}, u32[]{:S(2)}) copy-start(f32[256,256]{1,0:T(8,128)S(1)} %get-tuple-element.41) | copy-start | bytes 786436
  253.3 20.9 %copy-start.107 = (f32[256,16]{1,0:T(8,128)}, f32[256,16]{1,0:T(8,128)S(1)}, u32[]{:S(2)}) copy-start(f32[256,16]{1,0:T(8,128)S(1)} %get-tuple-element.99) | copy-start | bytes 49156
  253.3 20.9 %copy-start.49 = (f32[256,16]{1,0:T(8,128)}, f32[256,16]{1,0:T(8,128)S(1)}, u32[]{:S(2)}) copy-start(f32[256,16]{1,0:T(8,128)S(1)} %get-tuple-element.100) | copy-start | bytes 49156
  253.3 20.9 %copy-start.51 = (f32[256,16]{1,0:T(8,128)}, f32[256,16]{1,0:T(8,128)S(1)}, u32[]{:S(2)}) copy-start(f32[256,16]{1,0:T(8,128)S(1)} %get-tuple-element.101) | copy-start | bytes 49156
  253.3 20.9 %copy-start.53 = (f32[256,16]{1,0:T(8,128)}, f32[256,16]{1,0:T(8,128)S(1)}, u32[]{:S(2)}) copy-start(f32[256,16]{1,0:T(8,128)S(1)} %get-tuple-element.102) | copy-start | bytes 49156
  368.7 24.2 %copy-start.14 = (f32[64,16,256]{2,1,0:T(8,128)S(1)}, f32[64,16,256]{2,1,0:T(8,128)}, u32[]{:S(2)}) copy-start(f32[64,16,256]{2,1,0:T(8,128)} %add.355) | copy-start | bytes 3145732
  422.5 9.2 %copy-start.11 = (f32[128,16,256]{2,1,0:T(8,128)S(1)}, f32[128,16,256]{2,1,0:T(8,128)}, u32[]{:S(2)}) copy-start(f32[128,16,256]{2,1,0:T(8,128)} %add.357) | copy-start | bytes 6291460
  472.1 42.3 %copy-start.105 = (f32[256,16]{1,0:T(8,128)S(1)}, f32[256,16]{1,0:T(8,128)}, u32[]{:S(2)}) copy-start(f32[256,16]{1,0:T(8,128)} %get-tuple-element.107) | copy-start | bytes 49156
  531.2 9.9 %copy-start.110 = (f32[256,16]{1,0:T(8,128)S(1)}, f32[256,16]{1,0:T(8,128)}, u32[]{:S(2)}) copy-start(f32[256,16]{1,0:T(8,128)} %get-tuple-element.109) | copy-start | bytes 49156
  531.2 9.9 %copy-start.111 = (f32[256,16]{1,0:T(8,128)S(1)}, f32[256,16]{1,0:T(8,128)}, u32[]{:S(2)}) copy-start(f32[256,16]{1,0:T(8,128)} %get-tuple-element.110) | copy-start | bytes 49156
  531.2 9.9 %copy-start.112 = (f32[256,16]{1,0:T(8,128)S(1)}, f32[256,16]{1,0:T(8,128)}, u32[]{:S(2)}) copy-start(f32[256,16]{1,0:T(8,128)} %get-tuple-element.111) | copy-start | bytes 49156
  548.8 12.7 %copy-start.45 = (f32[256,16]{1,0:T(8,128)S(1)}, f32[256,16]{1,0:T(8,128)}, u32[]{:S(2)}) copy-start(f32[256,16]{1,0:T(8,128)} %get-tuple-element.98) | copy-start | bytes 49156
  548.8 12.7 %copy-start.47 = (f32[256,16]{1,0:T(8,128)S(1)}, f32[256,16]{1,0:T(8,128)}, u32[]{:S(2)}) copy-start(f32[256,16]{1,0:T(8,128)} %get-tuple-element.104) | copy-start | bytes 49156
  548.8 12.7 %copy-start.48 = (f32[256,16]{1,0:T(8,128)S(1)}, f32[256,16]{1,0:T(8,128)}, u32[]{:S(2)}) copy-start(f32[256,16]{1,0:T(8,128)} %get-tuple-element.105) | copy-start | bytes 49156
  548.8 12.7 %copy-start.50 = (f32[256,16]{1,0:T(8,128)S(1)}, f32[256,16]{1,0:T(8,128)}, u32[]{:S(2)}) copy-start(f32[256,16]{1,0:T(8,128)} %copy-done.49) | copy-start | bytes 49156
  548.8 12.7 %copy-start.57 = (f32[256,256]{1,0:T(8,128)S(1)}, f32[256,256]{1,0:T(8,128)}, u32[]{:S(2)}) copy-start(f32[256,256]{1,0:T(8,128)} %get-tuple-element.42) | copy-start | bytes 786436
  548.8 12.7 %copy-start.58 = (f32[256,256]{1,0:T(8,128)S(1)}, f32[256,256]{1,0:T(8,128)}, u32[]{:S(2)}) copy-start(f32[256,256]{1,0:T(8,128)} %get-tuple-element.46) | copy-start | bytes 786436
  548.9 12.7 %copy-start.59 = (f32[256,256]{1,0:T(8,128)S(1)}, f32[256,256]{1,0:T(8,128)}, u32[]{:S(2)}) copy-start(f32[256,256]{1,0:T(8,128)} %get-tuple-element.47) | copy-start | bytes 786436
  548.9 12.7 %copy-start.60 = (f32[256,256]{1,0:T(8,128)S(1)}, f32[256,256]{1,0:T(8,128)}, u32[]{:S(2)}) copy-start(f32[256,256]{1,0:T(8,128)} %get-tuple-element.48) | copy-start | bytes 786436
  548.9 12.7 %copy-start.61 = (f32[256,256]{1,0:T(8,128)S(1)}, f32[256,256]{1,0:T(8,128)}, u32[]{:S(2)}) copy-start(f32[256,256]{1,0:T(8,128)} %get-tuple-element.49) | copy-start | bytes 786436
  548.9 12.7 %copy-start.62 = (f32[256,256]{1,0:T(8,128)S(1)}, f32[256,256]{1,0:T(8,128)}, u32[]{:S(2)}) copy-start(f32[256,256]{1,0:T(8,128)} %get-tuple-element.50) | copy-start | bytes 786436
  548.9 12.7 %copy-start.104 = (f32[256,16]{1,0:T(8,128)S(1)}, f32[256,16]{1,0:T(8,128)}, u32[]{:S(2)}) copy-start(f32[256,16]{1,0:T(8,128)} %get-tuple-element.106) | copy-start | bytes 49156
  548.9 12.7 %copy-start.106 = (f32[256,16]{1,0:T(8,128)S(1)}, f32[256,16]{1,0:T(8,128)}, u32[]{:S(2)}) copy-start(f32[256,16]{1,0:T(8,128)} %get-tuple-element.107) | copy-start | bytes 49156
  561.6 9.6 %copy-start.94 = (f32[256,256]{1,0:T(8,128)S(1)}, f32[256,256]{1,0:T(8,128)}, u32[]{:S(2)}) copy-start(f32[256,256]{1,0:T(8,128)} %multiply_reduce_fusion.17) | copy-start | bytes 786436
  561.6 10.4 %copy-start.15 = (f32[256,16,256]{2,1,0:T(8,128)S(1)}, f32[256,16,256]{2,1,0:T(8,128)}, u32[]{:S(2)}) copy-start(f32[256,16,256]{2,1,0:T(8,128)} %get-tuple-element.40) | copy-start | bytes 12582916
  561.6 10.4 %copy-start.27 = (f32[256,256]{1,0:T(8,128)S(1)}, f32[256,256]{1,0:T(8,128)}, u32[]{:S(2)}) copy-start(f32[256,256]{1,0:T(8,128)} %get-tuple-element.81) | copy-start | bytes 786436
  561.6 10.4 %copy-start.29 = (f32[256,256]{1,0:T(8,128)S(1)}, f32[256,256]{1,0:T(8,128)}, u32[]{:S(2)}) copy-start(f32[256,256]{1,0:T(8,128)} %get-tuple-element.82) | copy-start | bytes 786436
  561.7 10.4 %copy-start.31 = (f32[256,256]{1,0:T(8,128)S(1)}, f32[256,256]{1,0:T(8,128)}, u32[]{:S(2)}) copy-start(f32[256,256]{1,0:T(8,128)} %get-tuple-element.83) | copy-start | bytes 786436
  561.7 10.4 %copy-start.33 = (f32[256,256]{1,0:T(8,128)S(1)}, f32[256,256]{1,0:T(8,128)}, u32[]{:S(2)}) copy-start(f32[256,256]{1,0:T(8,128)} %get-tuple-element.68) | copy-start | bytes 786436
  561.7 10.4 %copy-start.35 = (f32[256,256]{1,0:T(8,128)S(1)}, f32[256,256]{1,0:T(8,128)}, u32[]{:S(2)}) copy-start(f32[256,256]{1,0:T(8,128)} %get-tuple-element.69) | copy-start | bytes 786436
  561.7 10.4 %copy-start.37 = (f32[256,256]{1,0:T(8,128)S(1)}, f32[256,256]{1,0:T(8,128)}, u32[]{:S(2)}) copy-start(f32[256,256]{1,0:T(8,128)} %get-tuple-element.70) | copy-start | bytes 786436
  561.7 10.4 %copy-start.40 = (f32[256,16]{1,0:T(8,128)S(1)}, f32[256,16]{1,0:T(8,128)}, u32[]{:S(2)}) copy-start(f32[256,16]{1,0:T(8,128)} %copy-done.39) | copy-start | bytes 49156
  561.7 10.4 %copy-start.42 = (f32[256,16]{1,0:T(8,128)S(1)}, f32[256,16]{1,0:T(8,128)}, u32[]{:S(2)}) copy-start(f32[256,16]{1,0:T(8,128)} %get-tuple-element.122) | copy-start | bytes 49156
  561.7 10.4 %copy-start.44 = (f32[256,16]{1,0:T(8,128)S(1)}, f32[256,16]{1,0:T(8,128)}, u32[]{:S(2)}) copy-start(f32[256,16]{1,0:T(8,128)} %get-tuple-element.123) | copy-start | bytes 49156
  572.1 10.4 %copy-start.23 = (f32[256,256]{1,0:T(8,128)S(1)}, f32[256,256]{1,0:T(8,128)}, u32[]{:S(2)}) copy-start(f32[256,256]{1,0:T(8,128)} %get-tuple-element.22) | copy-start | bytes 786436
  572.1 11.2 %copy-start.22 = (f32[256,256]{1,0:T(8,128)S(1)}, f32[256,256]{1,0:T(8,128)}, u32[]{:S(2)}) copy-start(f32[256,256]{1,0:T(8,128)} %get-tuple-element.8) | copy-start | bytes 786436
  596.8 56.6 %copy-start.1 = (bf16[256,256]{1,0:T(8,128)(2,1)S(1)}, bf16[256,256]{1,0:T(8,128)(2,1)}, u32[]{:S(2)}) copy-start(bf16[256,256]{1,0:T(8,128)(2,1)} %param.16) | copy-start | bytes 393220
  (91 other events, 409.2 us)
Sparse Core Ops, SparseCore 0:
  9.8 87.7 all-gather.2
  102.1 102.2 all-gather.4
where the time goes:
time: 667 us; the launch traced here: 660 us
  local copies, waits for them, and re-layouts  226 us (34%)
  other arithmetic  167 us (25%)
  waiting for transfers between devices  150 us (22%)
  blocking collectives  55.1 us (8%)
  starting transfers between devices  33.6 us (5%)
  between operations  15.2 us (2%)
  matrix products  13.1 us (2%)
    pad x12, local copies, waits for them, and re-layouts, selective_scan(): _, through = lax.associative_scan(link_blocks, (totals, state), axis=0)  99.8 us
    all_gather x1, waiting for transfers between devices, local(): proj = lax.all_gather(local_proj, 'seq', axis=0, tiled=True)  88.2 us
    reduce_sum x8, other arithmetic, selective_scan(): local_parts.append(jnp.sum(c_now[:, :, None] * state, axis=1))  74.5 us
    all_gather x1, waiting for transfers between devices, local(): lax.all_gather(x_weight, 'seq', axis=0, tiled=True)  59.4 us
    all_to_all x1, blocking collectives, local(): return lax.all_to_all(gated, 'seq', split_axis=0, concat_axis=1, tiled=True)  55.1 us
    unnamed x267, local copies, waits for them, and re-layouts  46.1 us
    slice x1, local copies, waits for them, and re-layouts, selective_scan(): through[:blocks - 1]  40.5 us
    reduce_sum x2, other arithmetic, selective_scan(): jnp.sum(c_now[:, :, None] * jnp.exp(elapsed[place][:, None, :] * rate[Non...  17.5 us
  transfers between devices with their start and end apart: 6, of which 3 were waited for; matrix products, arithmetic and copies ran while one was open for 59% of the time, Pallas kernels for 0%

commit v1 on v0

--- a/solution.py
+++ b/solution.py
@@ -2,6 +2,12 @@
 import jax.numpy as jnp
 from jax import lax
 from jax.sharding import PartitionSpec as P
+
+
+def gather_by_exchange(x, axis, dim):
+    size = lax.axis_size(axis)
+    repeats = [size if d == dim else 1 for d in range(x.ndim)]
+    return lax.all_to_all(jnp.tile(x, repeats), axis, split_axis=dim, concat_axis=dim, tiled=True)
 
 
 def passed_along(value, axis, steps):
@@ -97,9 +103,7 @@
     params = gather_directly(jnp.concatenate([conv_weight, conv_bias[None, :]], 0), "seq", 1)
     outgoing = causal_conv(prior.astype(jnp.float32), conv_input, params[:width], params[width])
     local_proj = jnp.dot(
-        outgoing,
-        lax.all_gather(x_weight, "seq", axis=0, tiled=True),
-        preferred_element_type=jnp.float32,
+        outgoing, gather_by_exchange(x_weight, "seq", 0), preferred_element_type=jnp.float32
     )
     arrived, gate_part = (
         lax.all_to_all(outgoing, "seq", split_axis=1, concat_axis=0, tiled=True),

time: 667 us -> 725 us (1.087)
  waiting for transfers between devices: 150 us -> 192 us
  blocking collectives: 55.1 us -> 76 us
  other arithmetic: 167 us -> 159 us
    ppermute x1, waiting for transfers between devices: 0.01 us -> 96.7 us  [passed_along(): lax.ppermute(value, axis, [(source, source + steps) for source in range(i...]
    all_gather x1 -> x0, waiting for transfers between devices: 59.4 us -> none  [local(): lax.all_gather(x_weight, 'seq', axis=0, tiled=True)]
    all_to_all x0 -> x1, blocking collectives: none -> 20.9 us  [from_everyone(): return lax.all_to_all(copies, axis, split_axis=0, concat_axis=0, tiled=True)]
    unnamed x267 -> x269, local copies, waits for them, and re-layouts: 46.1 us -> 46.1 us
  transfers between devices with their start and end apart: 6 -> 5, of which waited for: 3 -> 3; matrix products, arithmetic and copies ran while one was open for 59% -> 53% of each run, Pallas kernels for 0% -> 0%
where the time goes in v1:
time: 725 us; the launch traced here: 713 us
  local copies, waits for them, and re-layouts  232 us (32%)
  waiting for transfers between devices  192 us (26%)
  other arithmetic  159 us (22%)
  blocking collectives  76 us (10%)
  starting transfers between devices  28.4 us (4%)
  between operations  15.5 us (2%)
  matrix products  10.9 us (2%)
    pad x12, local copies, waits for them, and re-layouts, selective_scan(): _, through = lax.associative_scan(link_blocks, (totals, state), axis=0)  99.8 us
    ppermute x1, waiting for transfers between devices, passed_along(): lax.ppermute(value, axis, [(source, source + steps) for source in range(i...  96.7 us
    all_gather x1, waiting for transfers between devices, local(): proj = lax.all_gather(local_proj, 'seq', axis=0, tiled=True)  92.1 us
    reduce_sum x8, other arithmetic, selective_scan(): local_parts.append(jnp.sum(c_now[:, :, None] * state, axis=1))  74.5 us
    all_to_all x1, blocking collectives, local(): return lax.all_to_all(gated, 'seq', split_axis=0, concat_axis=1, tiled=True)  55.1 us
    unnamed x269, local copies, waits for them, and re-layouts  46.1 us
    slice x1, local copies, waits for them, and re-layouts, selective_scan(): through[:blocks - 1]  40.5 us
    all_to_all x1, blocking collectives, from_everyone(): return lax.all_to_all(copies, axis, split_axis=0, concat_axis=0, tiled=True)  20.9 us
  transfers between devices with their start and end apart: 5, of which 3 were waited for; matrix products, arithmetic and copies ran while one was open for 53% of the time, Pallas kernels for 0%

profile of v1, /device:TPU:32, one launch (start us, length us, event | category | flops | bytes accessed | tf_op | source)
XLA Modules:
  0.0 713.1 jit_solution(1274582521403100421)
XLA Ops:
  7.9 20.9 %all_to_all.59 = bf16[32,5,256]{2,1,0:T(8,128)(2,1)S(1)} all-to-all(bf16[32,5,256]{2,1,0:T(8,128)(2,1)S(1)} %broadcast_in_dim.7), channel_id=1, replica_groups=mesh['seq'=32,'batch'=8] {'seq'}, dimensions={0} | all-to-all | bytes 163840 | tf_op jit(solution)/shard_map/all_to_all | solution.py:21
  28.9 3.6 tile.2
  32.5 5.3 all-to-all-start.1
  37.9 3.4 collective-permute-start
  41.7 96.7 %collective-permute-done = bf16[3,8192]{1,0:T(4,128)(2,1)S(1)} collective-permute-done((bf16[3,8192]{1,0:T(4,128)(2,1)S(1)}, bf16[3,8192]{1,0:T(4,128)(2,1)S(1)}, u32[]{:S(2)}, u32[]{:S(2)}) %collective-permute-start) | collective-permute-done | bytes 49184 | tf_op jit(solution)/shard_map/ppermute | solution.py:16
  138.6 2.9 multiply_convert_fusion.1
  141.5 3.3 all-to-all-done.1
  144.7 2.9 copy.40
  147.6 2.2 fusion.36
  151.4 9.6 %all-to-all-start.2 = ((bf16[128,32,256]{2,0,1:T(8,128)(2,1)}), bf16[128,32,256]{2,0,1:T(8,128)(2,1)S(1)}, u32[]{:S(2)}, u32[]{:S(2)}) async-start(bf16[128,32,256]{2,0,1:T(8,128)(2,1)} %bitcast.53), calls=%async_computation.2 | async-start | bytes 4194304 | tf_op jit(solution)/shard_map/all_to_all | solution.py:109
  161.0 3.2 copy.44
  164.2 92.1 %all-gather.2.cloned.1.call-done = f32[4096,288]{0,1:T(8,128)} async-done(((f32[128,288]{0,1:T(8,128)}), f32[4096,288]{0,1:T(8,128)}) %all-gather.2.cloned.1.call-update) | async-done | bytes 4718608 | tf_op jit(solution)/shard_map/all_gather | solution.py:112
  256.3 2.5 multiply_reduce_fusion.32
  258.9 10.0 %all-to-all-start.3 = ((bf16[128,32,256]{2,0,1:T(8,128)(2,1)}), bf16[128,32,256]{2,0,1:T(8,128)(2,1)}, u32[]{:S(2)}, u32[]{:S(2)}) async-start(bf16[128,32,256]{2,0,1:T(8,128)(2,1)} %bitcast.52), calls=%async_computation.3 | async-start | bytes 4194304 | tf_op jit(solution)/shard_map/all_to_all | solution.py:110
  268.9 8.7 %bitcast_multiply_fusion.2 = (f32[4096,256]{1,0:T(8,128)}, f32[4096,256]{1,0:T(8,128)}) fusion(bf16[128,32,256]{2,0,1:T(8,128)(2,1)S(1)} %all-to-all-done.2, f32[256]{0:T(256)S(1)} %copy-done.132, bf16[256,256]{1,0:T(8,128)(2,1)S(1)} %copy-done, f32[4096,288]{0,1:T(8,128)} %all-gather.2.cloned.1.call-done, f32[256]{0:T(256)S(1)} %copy-done.133, ...), kind=kOutput, calls=%fused_computation.23 | convolution fusion | flops 549453824 | bytes 14829568 | tf_op jit(solution)/shard_map/dot_general | solution.py:122
  277.6 5.0 reshape.174
  282.7 4.4 slice_add_fusion.22
  289.0 5.0 reshape.176
  294.0 4.0 fusion.30
  306.7 20.0 %multiply_reduce_fusion.1 = (f32[256,256]{1,0:T(8,128)}, f32[256,16,256]{2,1,0:T(8,128)S(1)}, f32[256,16,256]{2,1,0:T(8,128)S(1)}, f32[256,16,256]{2,1,0:T(8,128)}) fusion(f32[256,16]{1,0:T(8,128)S(1)} %get-tuple-element.99, f32[256,256]{1,0:T(8,128)} %get-tuple-element.77, f32[256,16]{1,0:T(8,128)} %get-tuple-element.117, ...), kind=kLoop, calls=%fused_computation.27 | loop fusion | flops 69140480 | bytes 21528576 | tf_op jit(solution)/shard_map/reduce_sum | solution.py:71
  326.8 6.3 multiply_reduce_fusion.3
  351.2 3.3 pad.55
  359.6 2.9 pad.57
  363.4 3.1 pad.56
  370.2 5.6 pad.58
  375.8 8.7 %pad.59 = f32[32,16,256]{2,1,0:T(8,128)} pad(f32[16,16,256]{2,1,0:T(8,128)} %add.351, f32[]{:T(128)} %constant.5.clone.1), padding=1_0_1x0_0_0x0_0_0 | pad | bytes 786436 | tf_op jit(solution)/shard_map/pad | solution.py:75
  386.6 2.3 fusion.20
  389.0 11.6 %pad.61 = f32[64,16,256]{2,1,0:T(8,128)S(1)} pad(f32[32,16,256]{2,1,0:T(8,128)} %add.353, f32[]{:T(128)} %constant.5.clone.1), padding=1_0_1x0_0_0x0_0_0 | pad | bytes 1572868 | tf_op jit(solution)/shard_map/pad | solution.py:75
  402.4 15.6 %pad.60 = f32[64,16,256]{2,1,0:T(8,128)} pad(f32[32,16,256]{2,1,0:T(8,128)} %pad_maximum_fusion.3, f32[]{:T(128)} %constant.5.clone.1), padding=0_1_1x0_0_0x0_0_0 | pad | bytes 1572868 | tf_op jit(solution)/shard_map/pad | solution.py:75
  418.0 2.1 fusion.19
  422.4 23.1 %pad.62 = f32[128,16,256]{2,1,0:T(8,128)S(1)} pad(f32[64,16,256]{2,1,0:T(8,128)} %pad_maximum_fusion.2, f32[]{:T(128)} %constant.5.clone.1), padding=0_1_1x0_0_0x0_0_0 | pad | bytes 3145732 | tf_op jit(solution)/shard_map/pad | solution.py:75
  445.6 20.5 %pad.63 = f32[128,16,256]{2,1,0:T(8,128)} pad(f32[64,16,256]{2,1,0:T(8,128)S(1)} %copy-done.14, f32[]{:T(128)} %constant.5.clone.1), padding=1_0_1x0_0_0x0_0_0 | pad | bytes 3145732 | tf_op jit(solution)/shard_map/pad | solution.py:75
  466.0 3.6 add.357
  470.2 4.1 fusion.18
  475.1 9.2 %multiply_reduce_fusion.17 = f32[256,256]{1,0:T(8,128)} fusion(f32[256,16]{1,0:T(8,128)S(1)} %copy-done.104, f32[256,256]{1,0:T(8,128)S(1)} %copy-done.94, f32[256,16]{1,0:T(8,128)S(1)} %copy-done.129, f32[256,256]{1,0:T(8,128)S(1)} %copy-done.103, f32[16,256]{1,0:T(8,128)S(1)} %exponential_negate_fusion, f32[256,256]{1,0:T(8,128)S(1)} %copy-done.93, ...), kind=kLoop, calls=%fused_computation.43 | loop fusion | flops 35586048 | bytes 4620288 | tf_op jit(solution)/shard_map/reduce_sum | solution.py:71
  484.3 40.5 %pad.161 = f32[256,16,256]{2,1,0:T(8,128)} pad(f32[128,16,256]{2,1,0:T(8,128)S(1)} %copy-done.11, f32[]{:T(128)} %constant.5.clone.1), padding=1_0_1x0_0_0x0_0_0 | pad | bytes 6291460
  526.6 40.5 %pad.87 = f32[255,16,256]{2,1,0:T(8,128)} pad(f32[128,16,256]{2,1,0:T(8,128)S(1)} %pad_maximum_fusion.1, f32[]{:T(128)} %constant.5.clone.1), padding=0_0_1x0_0_0x0_0_0 | pad | bytes 6275076 | tf_op jit(solution)/shard_map/slice | solution.py:76
  567.2 8.7 %multiply_reduce_fusion.19 = f32[256,256]{1,0:T(8,128)S(1)} fusion(f32[256,16]{1,0:T(8,128)S(1)} %copy-done.106, f32[256,256]{1,0:T(8,128)} %get-tuple-element.86, f32[256,16]{1,0:T(8,128)} %get-tuple-element.126, f32[256,256]{1,0:T(8,128)} %get-tuple-element.87, f32[256,16]{1,0:T(8,128)} %get-tuple-element.127, f32[256,256]{1,0:T(8,128)} %get-tuple-element.65, ...), kind=kLoop, calls=%fused_computation.45 | loop fusion | flops 31391744 | bytes 4079616 | tf_op jit(solution)/shard_map/reduce_sum | solution.py:71
  576.1 6.3 multiply_reduce_fusion.21
  583.9 9.1 %multiply_reduce_fusion.29 = (f32[256,256]{1,0:T(8,128)S(1)}, f32[256,256]{1,0:T(8,128)S(1)}, f32[256,256]{1,0:T(8,128)S(1)}, f32[256,256]{1,0:T(8,128)S(1)}, f32[256,256]{1,0:T(8,128)S(1)}, /*index=5*/f32[256,256]{1,0:T(8,128)S(1)}) fusion(f32[256,16]{1,0:T(8,128)S(1)} %copy-done.114, f32[256,256]{1,0:T(8,128)S(1)} %copy-done.88, ...), kind=kLoop, calls=%fused_computation.55 | loop fusion | flops 27918336 | bytes 7716864 | tf_op jit(solution)/shard_map/reduce_sum | solution.py:71
  593.8 7.5 %multiply_reduce_fusion.23 = (f32[256,256]{1,0:T(8,128)S(1)}, f32[256,256]{1,0:T(8,128)S(1)}, f32[256,256]{1,0:T(8,128)S(1)}) fusion(f32[256,16]{1,0:T(8,128)S(1)} %copy-done.111, f32[256,256]{1,0:T(8,128)S(1)} %copy-done.82, f32[256,16]{1,0:T(8,128)S(1)} %copy-done.118, f32[256,256]{1,0:T(8,128)S(1)} %copy-done.85, f32[256,16]{1,0:T(8,128)S(1)} %copy-done.120, ...), kind=kLoop, calls=%fused_computation.49 | loop fusion | flops 27066368 | bytes 3555328 | tf_op jit(solution)/shard_map/reduce_sum | solution.py:71
  601.6 8.8 %multiply_reduce_fusion = (f32[256,256]{1,0:T(8,128)S(1)}, f32[256,256]{1,0:T(8,128)S(1)}, f32[256,256]{1,0:T(8,128)S(1)}, f32[256,256]{1,0:T(8,128)S(1)}, f32[256,256]{1,0:T(8,128)S(1)}, /*index=5*/f32[256,256]{1,0:T(8,128)S(1)}) fusion(f32[256,16]{1,0:T(8,128)S(1)} %copy-done.109, f32[16,256]{1,0:T(8,128)S(1)} %exponential_negate_fusion, ...), kind=kLoop, calls=%fused_computation.26 | loop fusion | flops 24772608 | bytes 7438336 | tf_op jit(solution)/shard_map/reduce_sum | solution.py:80
  614.5 8.8 %multiply_reduce_fusion.2 = (f32[256,256]{1,0:T(8,128)S(1)}, f32[256,256]{1,0:T(8,128)S(1)}, f32[256,256]{1,0:T(8,128)S(1)}, f32[256,256]{1,0:T(8,128)S(1)}, f32[256,256]{1,0:T(8,128)S(1)}, /*index=5*/f32[256,256]{1,0:T(8,128)S(1)}) fusion(f32[256,256]{1,0:T(8,128)S(1)} %copy-done.58, f32[256,16]{1,0:T(8,128)S(1)} %copy-done.51, ...), kind=kLoop, calls=%fused_computation.28 | loop fusion | flops 24772608 | bytes 7438336 | tf_op jit(solution)/shard_map/reduce_sum | solution.py:80
  624.9 7.2 %multiply_reduce_fusion.9 = (f32[256,256]{1,0:T(8,128)S(1)}, f32[256,256]{1,0:T(8,128)S(1)}, f32[256,256]{1,0:T(8,128)S(1)}, f32[256,256]{1,0:T(8,128)S(1)}) fusion(f32[256,16]{1,0:T(8,128)S(1)} %copy-done.47, f32[256,256]{1,0:T(8,128)S(1)} %copy-done.28, f32[256,16]{1,0:T(8,128)S(1)} %copy-done.41, f32[256,256]{1,0:T(8,128)S(1)} %copy-done.38, ...), kind=kLoop, calls=%fused_computation.35 | loop fusion | flops 20709376 | bytes 6946816 | tf_op jit(solution)/shard_map/reduce_sum | solution.py:71
  638.3 4.9 reshape.177
  643.2 3.3 fusion.14
  646.6 2.9 fusion.15
  649.5 55.1 %all_to_all.60 = bf16[32,128,256]{2,1,0:T(8,128)(2,1)S(1)} all-to-all(bf16[32,128,256]{2,1,0:T(8,128)(2,1)S(1)} %bitcast.51), channel_id=1, replica_groups=mesh['seq'=32,'batch'=8] {'seq'}, dimensions={0} | all-to-all | bytes 4194304 | tf_op jit(solution)/shard_map/all_to_all | solution.py:132
  (342 shorter events, 66.3 us)
Async XLA Ops:
  6.5 262.4 %copy-start = (bf16[256,256]{1,0:T(8,128)(2,1)S(1)}, bf16[256,256]{1,0:T(8,128)(2,1)}, u32[]{:S(2)}) copy-start(bf16[256,256]{1,0:T(8,128)(2,1)} %param.16) | copy-start | bytes 393220
  32.5 112.2 %all-to-all-start.1 = ((bf16[32,256,288]{1,2,0:T(8,128)(2,1)}), bf16[32,256,288]{1,2,0:T(8,128)(2,1)}, u32[]{:S(2)}, u32[]{:S(2)}) async-start(bf16[32,256,288]{1,2,0:T(8,128)(2,1)} %tile.2), calls=%async_computation.1 | async-start | bytes 9437184 | tf_op jit(solution)/shard_map/all_to_all | solution.py:10
  37.8 218.5 %all-gather.2.cloned.1.call-start = ((), (), s32[]{:S(2)}) async-start(), calls=%async_computation.5 | async-start | bytes 4866048 | tf_op jit(solution)/shard_map/all_gather | solution.py:112
  37.9 100.5 %collective-permute-start = (bf16[3,8192]{1,0:T(4,128)(2,1)S(1)}, bf16[3,8192]{1,0:T(4,128)(2,1)S(1)}, u32[]{:S(2)}, u32[]{:S(2)}) collective-permute-start(bf16[3,8192]{1,0:T(4,128)(2,1)S(1)} %slice.443), channel_id=1, source_target_pairs={{0,8},{8,16},{16,24},{24,32},{32,40},{40,48},{48,56},{56,64},{64,7... | collective-permute-start | bytes 147464 | tf_op jit(solution)/shard_map/ppermute | solution.py:16
  151.4 12.8 %copy-start.130 = (f32[16,256]{1,0:T(8,128)S(1)}, f32[16,256]{1,0:T(8,128)}, u32[]{:S(2)}) copy-start(f32[16,256]{1,0:T(8,128)} %param.18) | copy-start | bytes 49156
  151.4 107.4 %all-to-all-start.2 = ((bf16[128,32,256]{2,0,1:T(8,128)(2,1)}), bf16[128,32,256]{2,0,1:T(8,128)(2,1)S(1)}, u32[]{:S(2)}, u32[]{:S(2)}) async-start(bf16[128,32,256]{2,0,1:T(8,128)(2,1)} %bitcast.53), calls=%async_computation.2 | async-start | bytes 4194304 | tf_op jit(solution)/shard_map/all_to_all | solution.py:109
  164.2 104.7 %copy-start.132 = (f32[256]{0:T(256)S(1)}, f32[256]{0:T(256)}, u32[]{:S(2)}) copy-start(f32[256]{0:T(256)} %param.17) | copy-start | bytes 3076
  164.2 104.7 %copy-start.133 = (f32[256]{0:T(256)S(1)}, f32[256]{0:T(256)}, u32[]{:S(2)}) copy-start(f32[256]{0:T(256)} %param.15) | copy-start | bytes 3076
  258.8 18.8 %copy-start.12 = (bf16[128,32,256]{2,0,1:T(8,128)(2,1)}, bf16[128,32,256]{2,0,1:T(8,128)(2,1)S(1)}, u32[]{:S(2)}) copy-start(bf16[128,32,256]{2,0,1:T(8,128)(2,1)S(1)} %all-to-all-done.2) | copy-start | bytes 6291460
  258.9 387.7 %all-to-all-start.3 = ((bf16[128,32,256]{2,0,1:T(8,128)(2,1)}), bf16[128,32,256]{2,0,1:T(8,128)(2,1)}, u32[]{:S(2)}, u32[]{:S(2)}) async-start(bf16[128,32,256]{2,0,1:T(8,128)(2,1)} %bitcast.52), calls=%async_computation.3 | async-start | bytes 4194304 | tf_op jit(solution)/shard_map/all_to_all | solution.py:110
  287.1 39.7 %copy-start.20 = (f32[256,256]{1,0:T(8,128)}, f32[256,256]{1,0:T(8,128)S(1)}, u32[]{:S(2)}) copy-start(f32[256,256]{1,0:T(8,128)S(1)} %get-tuple-element.41) | copy-start | bytes 786436
  305.9 20.9 %copy-start.108 = (f32[256,16]{1,0:T(8,128)}, f32[256,16]{1,0:T(8,128)S(1)}, u32[]{:S(2)}) copy-start(f32[256,16]{1,0:T(8,128)S(1)} %get-tuple-element.99) | copy-start | bytes 49156
  305.9 20.9 %copy-start.50 = (f32[256,16]{1,0:T(8,128)}, f32[256,16]{1,0:T(8,128)S(1)}, u32[]{:S(2)}) copy-start(f32[256,16]{1,0:T(8,128)S(1)} %get-tuple-element.100) | copy-start | bytes 49156
  305.9 20.9 %copy-start.52 = (f32[256,16]{1,0:T(8,128)}, f32[256,16]{1,0:T(8,128)S(1)}, u32[]{:S(2)}) copy-start(f32[256,16]{1,0:T(8,128)S(1)} %get-tuple-element.101) | copy-start | bytes 49156
  305.9 20.9 %copy-start.54 = (f32[256,16]{1,0:T(8,128)}, f32[256,16]{1,0:T(8,128)S(1)}, u32[]{:S(2)}) copy-start(f32[256,16]{1,0:T(8,128)S(1)} %get-tuple-element.102) | copy-start | bytes 49156
  421.3 24.2 %copy-start.14 = (f32[64,16,256]{2,1,0:T(8,128)S(1)}, f32[64,16,256]{2,1,0:T(8,128)}, u32[]{:S(2)}) copy-start(f32[64,16,256]{2,1,0:T(8,128)} %add.355) | copy-start | bytes 3145732
  475.1 9.2 %copy-start.11 = (f32[128,16,256]{2,1,0:T(8,128)S(1)}, f32[128,16,256]{2,1,0:T(8,128)}, u32[]{:S(2)}) copy-start(f32[128,16,256]{2,1,0:T(8,128)} %add.357) | copy-start | bytes 6291460
  524.8 42.3 %copy-start.106 = (f32[256,16]{1,0:T(8,128)S(1)}, f32[256,16]{1,0:T(8,128)}, u32[]{:S(2)}) copy-start(f32[256,16]{1,0:T(8,128)} %get-tuple-element.107) | copy-start | bytes 49156
  567.1 8.9 %copy-start.92 = (f32[256,256]{1,0:T(8,128)S(1)}, f32[256,256]{1,0:T(8,128)}, u32[]{:S(2)}) copy-start(f32[256,256]{1,0:T(8,128)} %get-tuple-element.87) | copy-start | bytes 786436
  583.8 9.9 %copy-start.111 = (f32[256,16]{1,0:T(8,128)S(1)}, f32[256,16]{1,0:T(8,128)}, u32[]{:S(2)}) copy-start(f32[256,16]{1,0:T(8,128)} %get-tuple-element.109) | copy-start | bytes 49156
  583.9 9.9 %copy-start.112 = (f32[256,16]{1,0:T(8,128)S(1)}, f32[256,16]{1,0:T(8,128)}, u32[]{:S(2)}) copy-start(f32[256,16]{1,0:T(8,128)} %get-tuple-element.110) | copy-start | bytes 49156
  583.9 9.9 %copy-start.113 = (f32[256,16]{1,0:T(8,128)S(1)}, f32[256,16]{1,0:T(8,128)}, u32[]{:S(2)}) copy-start(f32[256,16]{1,0:T(8,128)} %get-tuple-element.111) | copy-start | bytes 49156
  601.4 12.8 %copy-start.46 = (f32[256,16]{1,0:T(8,128)S(1)}, f32[256,16]{1,0:T(8,128)}, u32[]{:S(2)}) copy-start(f32[256,16]{1,0:T(8,128)} %get-tuple-element.98) | copy-start | bytes 49156
  601.4 12.8 %copy-start.48 = (f32[256,16]{1,0:T(8,128)S(1)}, f32[256,16]{1,0:T(8,128)}, u32[]{:S(2)}) copy-start(f32[256,16]{1,0:T(8,128)} %get-tuple-element.104) | copy-start | bytes 49156
  601.5 12.8 %copy-start.49 = (f32[256,16]{1,0:T(8,128)S(1)}, f32[256,16]{1,0:T(8,128)}, u32[]{:S(2)}) copy-start(f32[256,16]{1,0:T(8,128)} %get-tuple-element.105) | copy-start | bytes 49156
  601.5 12.8 %copy-start.51 = (f32[256,16]{1,0:T(8,128)S(1)}, f32[256,16]{1,0:T(8,128)}, u32[]{:S(2)}) copy-start(f32[256,16]{1,0:T(8,128)} %copy-done.50) | copy-start | bytes 49156
  601.5 12.8 %copy-start.58 = (f32[256,256]{1,0:T(8,128)S(1)}, f32[256,256]{1,0:T(8,128)}, u32[]{:S(2)}) copy-start(f32[256,256]{1,0:T(8,128)} %get-tuple-element.42) | copy-start | bytes 786436
  601.5 12.8 %copy-start.59 = (f32[256,256]{1,0:T(8,128)S(1)}, f32[256,256]{1,0:T(8,128)}, u32[]{:S(2)}) copy-start(f32[256,256]{1,0:T(8,128)} %get-tuple-element.46) | copy-start | bytes 786436
  601.5 12.8 %copy-start.60 = (f32[256,256]{1,0:T(8,128)S(1)}, f32[256,256]{1,0:T(8,128)}, u32[]{:S(2)}) copy-start(f32[256,256]{1,0:T(8,128)} %get-tuple-element.47) | copy-start | bytes 786436
  601.5 12.8 %copy-start.61 = (f32[256,256]{1,0:T(8,128)S(1)}, f32[256,256]{1,0:T(8,128)}, u32[]{:S(2)}) copy-start(f32[256,256]{1,0:T(8,128)} %get-tuple-element.48) | copy-start | bytes 786436
  601.5 12.8 %copy-start.62 = (f32[256,256]{1,0:T(8,128)S(1)}, f32[256,256]{1,0:T(8,128)}, u32[]{:S(2)}) copy-start(f32[256,256]{1,0:T(8,128)} %get-tuple-element.49) | copy-start | bytes 786436
  601.5 12.8 %copy-start.63 = (f32[256,256]{1,0:T(8,128)S(1)}, f32[256,256]{1,0:T(8,128)}, u32[]{:S(2)}) copy-start(f32[256,256]{1,0:T(8,128)} %get-tuple-element.50) | copy-start | bytes 786436
  601.5 12.8 %copy-start.105 = (f32[256,16]{1,0:T(8,128)S(1)}, f32[256,16]{1,0:T(8,128)}, u32[]{:S(2)}) copy-start(f32[256,16]{1,0:T(8,128)} %get-tuple-element.106) | copy-start | bytes 49156
  601.5 12.8 %copy-start.107 = (f32[256,16]{1,0:T(8,128)S(1)}, f32[256,16]{1,0:T(8,128)}, u32[]{:S(2)}) copy-start(f32[256,16]{1,0:T(8,128)} %get-tuple-element.107) | copy-start | bytes 49156
  614.4 9.7 %copy-start.95 = (f32[256,256]{1,0:T(8,128)S(1)}, f32[256,256]{1,0:T(8,128)}, u32[]{:S(2)}) copy-start(f32[256,256]{1,0:T(8,128)} %multiply_reduce_fusion.17) | copy-start | bytes 786436
  614.4 10.4 %copy-start.15 = (f32[256,16,256]{2,1,0:T(8,128)S(1)}, f32[256,16,256]{2,1,0:T(8,128)}, u32[]{:S(2)}) copy-start(f32[256,16,256]{2,1,0:T(8,128)} %get-tuple-element.40) | copy-start | bytes 12582916
  614.4 10.4 %copy-start.28 = (f32[256,256]{1,0:T(8,128)S(1)}, f32[256,256]{1,0:T(8,128)}, u32[]{:S(2)}) copy-start(f32[256,256]{1,0:T(8,128)} %get-tuple-element.81) | copy-start | bytes 786436
  614.4 10.4 %copy-start.30 = (f32[256,256]{1,0:T(8,128)S(1)}, f32[256,256]{1,0:T(8,128)}, u32[]{:S(2)}) copy-start(f32[256,256]{1,0:T(8,128)} %get-tuple-element.82) | copy-start | bytes 786436
  614.4 10.4 %copy-start.32 = (f32[256,256]{1,0:T(8,128)S(1)}, f32[256,256]{1,0:T(8,128)}, u32[]{:S(2)}) copy-start(f32[256,256]{1,0:T(8,128)} %get-tuple-element.83) | copy-start | bytes 786436
  614.4 10.4 %copy-start.34 = (f32[256,256]{1,0:T(8,128)S(1)}, f32[256,256]{1,0:T(8,128)}, u32[]{:S(2)}) copy-start(f32[256,256]{1,0:T(8,128)} %get-tuple-element.68) | copy-start | bytes 786436
  614.4 10.4 %copy-start.36 = (f32[256,256]{1,0:T(8,128)S(1)}, f32[256,256]{1,0:T(8,128)}, u32[]{:S(2)}) copy-start(f32[256,256]{1,0:T(8,128)} %get-tuple-element.69) | copy-start | bytes 786436
  614.4 10.4 %copy-start.38 = (f32[256,256]{1,0:T(8,128)S(1)}, f32[256,256]{1,0:T(8,128)}, u32[]{:S(2)}) copy-start(f32[256,256]{1,0:T(8,128)} %get-tuple-element.70) | copy-start | bytes 786436
  614.4 10.4 %copy-start.41 = (f32[256,16]{1,0:T(8,128)S(1)}, f32[256,16]{1,0:T(8,128)}, u32[]{:S(2)}) copy-start(f32[256,16]{1,0:T(8,128)} %copy-done.40) | copy-start | bytes 49156
  614.4 10.4 %copy-start.43 = (f32[256,16]{1,0:T(8,128)S(1)}, f32[256,16]{1,0:T(8,128)}, u32[]{:S(2)}) copy-start(f32[256,16]{1,0:T(8,128)} %get-tuple-element.122) | copy-start | bytes 49156
  614.5 10.4 %copy-start.45 = (f32[256,16]{1,0:T(8,128)S(1)}, f32[256,16]{1,0:T(8,128)}, u32[]{:S(2)}) copy-start(f32[256,16]{1,0:T(8,128)} %get-tuple-element.123) | copy-start | bytes 49156
  624.9 10.3 %copy-start.24 = (f32[256,256]{1,0:T(8,128)S(1)}, f32[256,256]{1,0:T(8,128)}, u32[]{:S(2)}) copy-start(f32[256,256]{1,0:T(8,128)} %get-tuple-element.22) | copy-start | bytes 786436
  624.9 11.0 %copy-start.23 = (f32[256,256]{1,0:T(8,128)S(1)}, f32[256,256]{1,0:T(8,128)}, u32[]{:S(2)}) copy-start(f32[256,256]{1,0:T(8,128)} %get-tuple-element.8) | copy-start | bytes 786436
  649.4 56.6 %copy-start.1 = (bf16[256,256]{1,0:T(8,128)(2,1)S(1)}, bf16[256,256]{1,0:T(8,128)(2,1)}, u32[]{:S(2)}) copy-start(bf16[256,256]{1,0:T(8,128)(2,1)} %param.16) | copy-start | bytes 393220
  (91 other events, 405.5 us)
Sparse Core Ops, SparseCore 0:
  149.9 106.2 all-gather.1
